TPU v7x, 32 devices: a whole 2x2x4 slice. The times are simulated.
32 devices in a mesh: seq: 8 (over z, core), tp: 4 (over y, x).
Axes of the slice: x: 2, y: 2, z: 4, core: 2. Of those that a mesh axis runs over, the one named last changes fastest.
Arguments:
- tokens: bfloat16 [1024, 8192], P('seq'), may hold values from -6 to 6
- conv_weight: float32 [4, 8192], replicated, may hold values from -3 to 3
- norm_gain: float32 [8192], replicated, may hold values from 0.25 to 1.75
- gate_weight: bfloat16 [8192, 14336], P('seq', 'tp'), may hold values from -0.0625 to 0.0625
- up_weight: bfloat16 [8192, 14336], P('seq', 'tp'), may hold values from -0.0625 to 0.0625
- down_weight: bfloat16 [14336, 8192], P('tp', 'seq'), may hold values from -0.046875 to 0.046875
Outputs:
- mixed_out: bfloat16 [1024, 8192], P(('seq', 'tp'))
All inputs are finite; a program needn't handle non-finite values.
Results may differ from a plain program's by a relative error of at most 0.03.
Values may be sent and summed in bfloat16 or wider, within the bound.
A program may use at most 128 MiB of HBM per device.

v0:
```python
import jax
import jax.numpy as jnp
from jax import lax
from jax.sharding import PartitionSpec as P


def from_behind(shard, axis, by):
    peers = lax.axis_size(axis)
    pairs = [(i, i + by) for i in range(peers) if 0 <= i + by < peers]
    return lax.ppermute(shard, axis, pairs)


def swiglu(both_sums, half_cols):
    return (jax.nn.silu(both_sums[:, :half_cols]) * both_sums[:, half_cols:]).astype(jnp.bfloat16)


def shards(tokens, conv_weight, norm_gain, gate_weight, up_weight, down_weight):
    tok_rows = tokens.shape[0]
    taps_count = conv_weight.shape[0]
    seq_count = lax.axis_size("seq")
    edge_rows = from_behind(tokens[tok_rows - (taps_count - 1) :], "seq", 1)
    extended = jnp.concatenate([edge_rows, tokens], 0).astype(jnp.float32)
    conv_out = jnp.zeros(tokens.shape, jnp.float32)
    for tap_index in range(taps_count):
        begin = taps_count - 1 - tap_index
        conv_out = conv_out + conv_weight[tap_index][None, :] * extended[begin : begin + tok_rows]
    scale_rms = lax.rsqrt(jnp.mean(conv_out * conv_out, axis=-1, keepdims=True) + 1e-05)
    normed = (conv_out * scale_rms * norm_gain[None, :]).astype(jnp.bfloat16)
    all_rows = lax.all_to_all(normed, "seq", split_axis=1, concat_axis=0, tiled=True)
    half_cols = gate_weight.shape[1]
    w_both = jnp.concatenate([gate_weight, up_weight], 1)
    gate_share = lax.psum_scatter(
        jnp.dot(all_rows, w_both, preferred_element_type=jnp.float32).astype(jnp.bfloat16),
        "seq",
        scatter_dimension=0,
        tiled=True,
    ).astype(jnp.float32)
    hidden = swiglu(gate_share, half_cols)
    out_terms = jnp.dot(
        lax.all_gather(hidden, "seq", axis=0, tiled=True),
        down_weight,
        preferred_element_type=jnp.float32,
    )
    col_width = out_terms.shape[1]
    out_terms = out_terms.reshape(seq_count, tok_rows, col_width)
    summed = lax.psum_scatter(out_terms.astype(jnp.bfloat16), "tp", scatter_dimension=1, tiled=True)
    mixed_out = lax.all_to_all(summed, "seq", split_axis=0, concat_axis=2, tiled=True)
    return mixed_out.reshape(mixed_out.shape[1], mixed_out.shape[2])


def solution(mesh):
    in_specs = (P("seq", None), P(), P(), P("seq", "tp"), P("seq", "tp"), P("tp", "seq"))
    out_specs = P(("seq", "tp"), None)
    return jax.shard_map(shards, mesh=mesh, in_specs=in_specs, out_specs=out_specs, check_vma=False)
```

profile of v0, /device:TPU:0, one launch (start us, length us, event | category | flops | bytes accessed | tf_op | source)
XLA Modules:
  0.0 409.3 jit_solution(17760382771565718284)
XLA Ops:
  6.5 0.0 reduce-scatter.3.cloned.1.call-start
  6.5 0.9 slice.34
  7.5 2.4 collective-permute-start
  9.9 1.3 fusion.13
  11.2 3.2 copy.14
  14.4 0.0 collective-permute-done
  14.4 1.9 copy.13
  16.3 3.1 maximum_convert_fusion
  19.4 0.0 copy-start
  19.4 8.7 %multiply_reduce_fusion = (f32[128]{0:T(128)S(1)}, f32[128,8192]{0,1:T(8,128)S(1)}) fusion(f32[131,8192]{0,1:T(8,128)S(1)} %maximum_convert_fusion, f32[8192]{0:T(1024)S(1)} %bitcast.26, f32[8192]{0:T(1024)S(1)} %bitcast.27, f32[8192]{0:T(1024)S(1)} %bitcast.25, f32[8192]{0:T(1024)S(1)} %bitcast.24), kind=kLoop, calls=%fused_computation.14 | loop fusion | flops 9437056 | bytes 21103104 | tf_op jit(solution)/shard_map/reduce_sum | solution.py:27
  28.1 0.0 copy-done
  28.2 3.5 multiply_convert_fusion
  31.6 55.0 %all_to_all.34 = bf16[128,8,1024]{0,2,1:T(8,128)(2,1)S(1)} all-to-all(bf16[128,8,1024]{0,2,1:T(8,128)(2,1)S(1)} %bitcast.19), channel_id=1, replica_groups=mesh['seq'=8,'tp'=4] {'seq'}, dimensions={1} | all-to-all | bytes 4194304 | tf_op jit(solution)/shard_map/all_to_all | solution.py:29
  86.6 2.6 copy.15
  89.2 22.3 %fusion.4 = bf16[1024,7168]{1,0:T(8,128)(2,1)} fusion(bf16[1024,1024]{1,0:T(8,128)(2,1)} %bitcast.22, bf16[1024,3584]{1,0:T(8,128)(2,1)} %param.10, bf16[1024,3584]{1,0:T(8,128)(2,1)} %param.9), kind=kOutput, calls=%fused_computation.4 | convolution fusion | flops 15069085696 | bytes 31457280 | tf_op jit(solution)/shard_map/dot_general | solution.py:33
  111.6 0.0 reduce-scatter.3.cloned.1.call-update
  111.6 0.0 all-gather.2.cloned.1.call-start
  111.6 148.0 %reduce-scatter.3.cloned.1.call-done = bf16[128,7168]{1,0:T(8,128)(2,1)} async-done(((bf16[1024,7168]{1,0:T(8,128)(2,1)}), bf16[128,7168]{1,0:T(8,128)(2,1)}) %reduce-scatter.3.cloned.1.call-update) | async-done | bytes 1835024 | tf_op jit(solution)/shard_map/reduce_scatter | solution.py:32
  259.6 1.9 convert_element_type.24
  261.5 1.4 fusion.10
  262.9 0.0 all-gather.2.cloned.1.call-update
  263.0 0.0 reduce-scatter.5.cloned.1.call-start
  263.0 71.9 %all-gather.2.cloned.1.call-done = bf16[1024,3584]{1,0:T(8,128)(2,1)} async-done(((bf16[128,3584]{1,0:T(8,128)(2,1)}), bf16[1024,3584]{1,0:T(8,128)(2,1)}) %all-gather.2.cloned.1.call-update) | async-done | bytes 7340048 | tf_op jit(solution)/shard_map/all_gather | solution.py:40
  334.9 13.2 %convolution_convert_fusion = bf16[1024,1024]{1,0:T(8,128)(2,1)} fusion(bf16[1024,3584]{1,0:T(8,128)(2,1)} %all-gather.2.cloned.1.call-done, bf16[3584,1024]{1,0:T(8,128)(2,1)} %param.11), kind=kOutput, calls=%fused_computation.15 | convolution fusion | flops 7517241344 | bytes 16777216 | tf_op jit(solution)/shard_map/dot_general | solution.py:39
  348.1 0.0 reduce-scatter.5.cloned.1.call-update
  348.1 33.9 %reduce-scatter.5.cloned.1.call-done = bf16[8,32,1024]{2,1,0:T(8,128)(2,1)} async-done(((bf16[8,128,1024]{2,1,0:T(8,128)(2,1)}), bf16[8,32,1024]{2,1,0:T(8,128)(2,1)}) %reduce-scatter.5.cloned.1.call-update) | async-done | bytes 524304 | tf_op jit(solution)/shard_map/reduce_scatter | solution.py:46
  382.1 19.9 %all_to_all.35 = bf16[8,32,1024]{2,1,0:T(8,128)(2,1)S(1)} all-to-all(bf16[8,32,1024]{2,1,0:T(8,128)(2,1)} %reduce-scatter.5.cloned.1.call-done), channel_id=1, replica_groups=mesh['seq'=8,'tp'=4] {'seq'}, dimensions={0} | all-to-all | bytes 1048576 | tf_op jit(solution)/shard_map/all_to_all | solution.py:47
  402.0 0.8 copy.17
  (1 shorter events, 0.0 us)
Async XLA Ops:
  6.5 253.1 %reduce-scatter.3.cloned.1.call-start = ((), (), s32[]{:S(2)}) async-start(), calls=%async_computation.4 | async-start | bytes 16515072 | tf_op jit(solution)/shard_map/reduce_scatter | solution.py:32
  7.5 6.9 %collective-permute-start = (bf16[3,8192]{1,0:T(4,128)(2,1)S(1)}, bf16[3,8192]{1,0:T(4,128)(2,1)S(1)}, u32[]{:S(2)}, u32[]{:S(2)}) collective-permute-start(bf16[3,8192]{1,0:T(4,128)(2,1)S(1)} %slice.34), channel_id=1, source_target_pairs={{0,4},{4,8},{8,12},{12,16},{16,20},{20,24},{24,28},{1,5},{5,9},{9,... | collective-permute-start | bytes 147464 | tf_op jit(solution)/shard_map/ppermute | solution.py:10
  19.4 8.8 %copy-start = (f32[8192]{0:T(1024)S(1)}, f32[8192]{0:T(1024)}, u32[]{:S(2)}) copy-start(f32[8192]{0:T(1024)} %param.8) | copy-start | bytes 98308
  111.6 223.3 %all-gather.2.cloned.1.call-start = ((), (), s32[]{:S(2)}) async-start(), calls=%async_computation.5 | async-start | bytes 8257536 | tf_op jit(solution)/shard_map/all_gather | solution.py:40
  263.0 119.1 %reduce-scatter.5.cloned.1.call-start = ((), (), s32[]{:S(2)}) async-start(), calls=%async_computation.6 | async-start | bytes 2621440 | tf_op jit(solution)/shard_map/reduce_scatter | solution.py:46
Sparse Core Ops, SparseCore 0:
  111.7 147.8 reduce-scatter.2
  263.1 71.8 all-gather.1
  348.3 33.7 reduce-scatter.4
where the time goes:
time: 410 us; the launch traced here: 409 us
  waiting for transfers between devices  254 us (62%)
  blocking collectives  74.9 us (18%)
  matrix products  35.5 us (9%)
  other arithmetic  18.6 us (5%)
  between operations  13.2 us (3%)
  local copies, waits for them, and re-layouts  10.8 us (3%)
    reduce_scatter x1, waiting for transfers between devices, shards(): lax.psum_scatter(jnp.dot(all_rows, w_both, preferred_element_type=jnp.flo...  148 us
    all_gather x1, waiting for transfers between devices, shards(): lax.all_gather(hidden, 'seq', axis=0, tiled=True)  71.9 us
    all_to_all x1, blocking collectives, shards(): lax.all_to_all(normed, 'seq', split_axis=1, concat_axis=0, tiled=True)  55 us
    reduce_scatter x1, waiting for transfers between devices, shards(): lax.psum_scatter(out_terms.astype(jnp.bfloat16), 'tp', scatter_dimension=...  33.9 us
    dot_general x1, matrix products, shards(): jnp.dot(all_rows, w_both, preferred_element_type=jnp.float32)  22.3 us
    all_to_all x1, blocking collectives, shards(): lax.all_to_all(summed, 'seq', split_axis=0, concat_axis=2, tiled=True)  19.9 us
    dot_general x1, matrix products, shards(): jnp.dot(lax.all_gather(hidden, 'seq', axis=0, tiled=True), down_weight, p...  13.2 us
    reduce_sum x1, other arithmetic, shards(): jnp.mean(conv_out * conv_out, axis=-1, keepdims=True) + 1e-05  8.75 us
  transfers between devices with their start and end apart: 4, of which 3 were waited for; matrix products, arithmetic and copies ran while one was open for 1% of the time, Pallas kernels for 0%

commit v1 on v0

v1 whole, which is shorter than its diff:
```python
import functools

import jax
import jax.numpy as jnp
from jax import lax
from jax.experimental import pallas as pl
from jax.experimental.pallas import tpu as pltpu
from jax.sharding import PartitionSpec as P

MESH = pl.DeviceIdType.MESH
WIDTH = 256
BLOCK_TOKENS = 1024
RS_LAG = 1
AG_LAG = 1


def from_behind(shard, axis, by):
    peers = lax.axis_size(axis)
    pairs = [(i, i + by) for i in range(peers) if 0 <= i + by < peers]
    return lax.ppermute(shard, axis, pairs)


def ffn_kernel(seq_n, tp_n, x_ref, gw_ref, uw_ref, dw_ref, out_ref, x_all, w_buf, d_buf, own, give, got, chain, hid, acc,
               x_snd, x_rcv, x_loc, w_sem, d_sem, p_snd, p_rcv, c_snd, c_rcv, h_snd, h_rcv, q_snd, q_rcv):
    stops = seq_n // 2
    seq_i = lax.axis_index("seq")
    tp_i = lax.axis_index("tp")
    pos = seq_i // 2
    core = seq_i % 2
    partner = (pos * 2 + 1 - core, tp_i)

    def at_stop(stop):
        return (stop * 2 + core, tp_i)

    sub = x_ref.shape[0]
    tokens = sub * tp_n
    half = tokens // 2
    quarter = half // 2
    chunks = gw_ref.shape[1] // WIDTH

    def w_copies(c):
        slot = c % 2
        cols = pl.ds(pl.multiple_of(c * WIDTH, WIDTH), WIDTH)
        return [
            pltpu.make_async_copy(gw_ref.at[:, cols], w_buf.at[slot, 0], w_sem.at[slot, 0]),
            pltpu.make_async_copy(uw_ref.at[:, cols], w_buf.at[slot, 1], w_sem.at[slot, 1]),
        ]

    for c in range(2):
        for cp in w_copies(c):
            cp.start()
    d_copy = pltpu.make_async_copy(dw_ref, d_buf, d_sem)
    d_copy.start()
    my_x = pl.ds(pl.multiple_of(tp_i * sub, sub), sub)
    x_own = pltpu.make_async_copy(x_ref, x_all.at[my_x], x_loc)
    x_own.start()

    barrier = pltpu.get_barrier_semaphore()
    greet = [partner, at_stop((pos + 1) % stops), at_stop((pos + stops - 1) % stops)]
    greet += [(seq_i, (tp_i + j) % tp_n) for j in range(1, tp_n)]
    for dev in greet:
        pl.semaphore_signal(barrier, inc=1, device_id=dev, device_id_type=MESH)
    pl.semaphore_wait(barrier, len(greet))

    def x_copy(j):
        return pltpu.make_async_remote_copy(
            src_ref=x_ref, dst_ref=x_all.at[my_x], send_sem=x_snd.at[j], recv_sem=x_rcv.at[j],
            device_id=(seq_i, (tp_i + j + 1) % tp_n), device_id_type=MESH)

    def x_land(j):
        origin = (tp_i + tp_n - j - 1) % tp_n
        rows = pl.ds(pl.multiple_of(origin * sub, sub), sub)
        return pltpu.make_async_remote_copy(
            src_ref=x_ref, dst_ref=x_all.at[rows], send_sem=x_snd.at[j], recv_sem=x_rcv.at[j],
            device_id=(seq_i, (tp_i + j + 1) % tp_n), device_id_type=MESH)

    for j in range(tp_n - 1):
        x_copy(j).start()
    acc[...] = jnp.zeros_like(acc)
    x_own.wait()
    for j in range(tp_n - 1):
        x_land(j).wait_recv()

    def swap_copy(c, h):
        return pltpu.make_async_remote_copy(
            src_ref=give.at[c, h], dst_ref=got.at[c, h], send_sem=p_snd.at[h, c], recv_sem=p_rcv.at[h, c],
            device_id=partner, device_id_type=MESH)

    def step_of(h):
        return -1 if h == 0 else 1

    def clamp(stop):
        return jnp.clip(stop, 0, stops - 1)

    def chain_copy(c, h):
        return pltpu.make_async_remote_copy(
            src_ref=got.at[c, h], dst_ref=chain.at[c, h], send_sem=c_snd.at[h, c], recv_sem=c_rcv.at[h, c],
            device_id=at_stop(pos + step_of(h)), device_id_type=MESH)

    def back_copy(c, h):
        return pltpu.make_async_remote_copy(
            src_ref=hid.at[c, h, core], dst_ref=hid.at[c, h, core], send_sem=h_snd.at[h, c], recv_sem=h_rcv.at[h, c],
            device_id=at_stop(pos - step_of(h)), device_id_type=MESH)

    def side_copy(c, h):
        return pltpu.make_async_remote_copy(
            src_ref=hid.at[c, h, core], dst_ref=hid.at[c, h, core], send_sem=q_snd.at[h, c], recv_sem=q_rcv.at[h, c],
            device_id=partner, device_id_type=MESH)

    def side_land(c, h):
        return pltpu.make_async_remote_copy(
            src_ref=hid.at[c, h, 1 - core], dst_ref=hid.at[c, h, 1 - core], send_sem=q_snd.at[h, c],
            recv_sem=q_rcv.at[h, c], device_id=partner, device_id_type=MESH)

    def done_before(h):
        return stops - 1 - pos if h == 0 else pos

    def inside(c):
        return jnp.logical_and(c >= 0, c < chunks)

    def multiply(c):
        slot = c % 2
        for cp in w_copies(c):
            cp.wait()
        for h in range(2):
            for mine in range(2):
                q = core if mine else 1 - core
                rows = x_all[pl.ds(pl.multiple_of(h * half + q * quarter, quarter), quarter), :]
                dest = own if mine else give
                for k in range(2):
                    part = jnp.dot(rows, w_buf[slot, k], preferred_element_type=jnp.float32)
                    dest[c, h, :, k * WIDTH : (k + 1) * WIDTH] = part.astype(jnp.bfloat16)
        for h in range(2):
            swap_copy(c, h).start()

        @pl.when(c + 2 < chunks)
        def _():
            for cp in w_copies(c + 2):
                cp.start()

    def reduce(c, h):
        swap_copy(c, h).wait_recv()
        before = done_before(h)
        total = lambda: own[c, h].astype(jnp.float32) + got[c, h].astype(jnp.float32)

        @pl.when(before == 0)
        def _():
            got[c, h] = total().astype(jnp.bfloat16)

        @pl.when(before > 0)
        def _():
            chain_copy(c, h).wait_recv()

        @pl.when(jnp.logical_and(before > 0, before < stops - 1))
        def _():
            got[c, h] = (total() + chain[c, h].astype(jnp.float32)).astype(jnp.bfloat16)

        @pl.when(before < stops - 1)
        def _():
            chain_copy(c, h).start()

        @pl.when(before == stops - 1)
        def _():
            both = total() + chain[c, h].astype(jnp.float32)
            gate = both[:, :WIDTH]
            hid[c, h, core] = (gate / (1.0 + jnp.exp(-gate)) * both[:, WIDTH:]).astype(jnp.bfloat16)
            back_copy(c, h).start()
            side_copy(c, h).start()

    def relay(c, h):
        before = done_before(h)

        @pl.when(before < stops - 1)
        def _():
            back_copy(c, h).wait_recv()

            @pl.when(before > 0)
            def _():
                back_copy(c, h).start()

            side_copy(c, h).start()

    def down(c, h):
        side_land(c, h).wait_recv()
        d_rows = d_buf[pl.ds(pl.multiple_of(c * WIDTH, WIDTH), WIDTH), :]
        for q in range(2):
            rows = slice(h * half + q * quarter, h * half + (q + 1) * quarter)
            acc[rows, :] += jnp.dot(hid[c, h, q], d_rows, preferred_element_type=jnp.float32)

    @pl.loop(0, chunks + 2 + (RS_LAG + AG_LAG) * (stops - 1))
    def _(t):
        rs_c = [t - 1 - RS_LAG * done_before(h) for h in range(2)]
        ag_c = [t - 1 - RS_LAG * (stops - 1) - AG_LAG * (stops - 1 - done_before(h)) for h in range(2)]

        for h in range(2):
            @pl.when(inside(rs_c[h]))
            def _(h=h):
                reduce(rs_c[h], h)

        for h in range(2):
            @pl.when(inside(ag_c[h]))
            def _(h=h):
                relay(ag_c[h], h)

        @pl.when(t < chunks)
        def _():
            multiply(t)

        @pl.when(t == 1 + RS_LAG * (stops - 1))
        def _():
            d_copy.wait()

        for h in range(2):
            @pl.when(inside(ag_c[h] - 1))
            def _(h=h):
                down(ag_c[h] - 1, h)

    out_ref[...] = acc[...].astype(out_ref.dtype)

    for j in range(tp_n - 1):
        x_copy(j).wait_send()

    @pl.loop(0, chunks)
    def _(c):
        for h in range(2):
            before = done_before(h)
            swap_copy(c, h).wait_send()
            side_copy(c, h).wait_send()

            @pl.when(before < stops - 1)
            def _(h=h):
                chain_copy(c, h).wait_send()

            @pl.when(before > 0)
            def _(h=h):
                back_copy(c, h).wait_send()


def ffn(x_sub, gate_weight, up_weight, down_weight, call):
    seq_n, tp_n = lax.axis_size("seq"), lax.axis_size("tp")
    sub, feats = x_sub.shape
    units = gate_weight.shape[1]
    cols = down_weight.shape[1]
    tokens = sub * tp_n
    quarter = tokens // 4
    n = units // WIDTH
    bf16 = jnp.bfloat16
    dma = pltpu.SemaphoreType.DMA
    vmem = pl.BlockSpec(memory_space=pltpu.VMEM)
    anywhere = pl.BlockSpec(memory_space=pl.ANY)
    return pl.pallas_call(
        functools.partial(ffn_kernel, seq_n, tp_n),
        out_shape=jax.ShapeDtypeStruct((tokens, cols), bf16),
        in_specs=[vmem, anywhere, anywhere, anywhere],
        out_specs=vmem,
        scratch_shapes=[
            pltpu.VMEM((tokens, feats), bf16),
            pltpu.VMEM((2, 2, feats, WIDTH), bf16),
            pltpu.VMEM((units, cols), bf16),
            pltpu.VMEM((n, 2, quarter, 2 * WIDTH), bf16),
            pltpu.VMEM((n, 2, quarter, 2 * WIDTH), bf16),
            pltpu.VMEM((n, 2, quarter, 2 * WIDTH), bf16),
            pltpu.VMEM((n, 2, quarter, 2 * WIDTH), bf16),
            pltpu.VMEM((n, 2, 2, quarter, WIDTH), bf16),
            pltpu.VMEM((tokens, cols), jnp.float32),
            dma((tp_n - 1,)), dma((tp_n - 1,)), dma(()), dma((2, 2)), dma(()),
            dma((2, n)), dma((2, n)), dma((2, n)), dma((2, n)), dma((2, n)), dma((2, n)), dma((2, n)), dma((2, n)),
        ],
        compiler_params=pltpu.CompilerParams(
            collective_id=call, has_side_effects=True, vmem_limit_bytes=63 * 1024 * 1024),
        cost_estimate=pl.CostEstimate(
            flops=6 * tokens * feats * units, bytes_accessed=6 * feats * units, transcendentals=0),
    )(x_sub, gate_weight, up_weight, down_weight)


def shards(tokens, conv_weight, norm_gain, gate_weight, up_weight, down_weight):
    tok_rows = tokens.shape[0]
    taps_count = conv_weight.shape[0]
    seq_count = lax.axis_size("seq")
    tp_count = lax.axis_size("tp")
    part_rows = tok_rows // tp_count
    edge_rows = from_behind(tokens[tok_rows - (taps_count - 1) :], "seq", 1)
    extended = jnp.concatenate([edge_rows, tokens], 0)
    extended = lax.dynamic_slice_in_dim(
        extended, lax.axis_index("tp") * part_rows, part_rows + taps_count - 1, 0).astype(jnp.float32)
    conv_out = jnp.zeros((part_rows, tokens.shape[1]), jnp.float32)
    for tap_index in range(taps_count):
        begin = taps_count - 1 - tap_index
        conv_out = conv_out + conv_weight[tap_index][None, :] * extended[begin : begin + part_rows]
    scale_rms = lax.rsqrt(jnp.mean(conv_out * conv_out, axis=-1, keepdims=True) + 1e-05)
    normed = (conv_out * scale_rms * norm_gain[None, :]).astype(jnp.bfloat16)
    x_sub = lax.all_to_all(normed, "seq", split_axis=1, concat_axis=0, tiled=True)
    blocks = max(1, x_sub.shape[0] * tp_count // BLOCK_TOKENS)
    rows = x_sub.shape[0] // blocks
    parts = [
        ffn(x_sub[b * rows : (b + 1) * rows], gate_weight, up_weight, down_weight, b).reshape(tp_count, rows, -1)
        for b in range(blocks)
    ]
    terms = parts[0] if blocks == 1 else jnp.concatenate(parts, 1)
    pieces = lax.all_to_all(terms, "tp", split_axis=0, concat_axis=0, tiled=True)
    summed = jnp.sum(pieces.astype(jnp.float32), 0).astype(jnp.bfloat16)
    summed = summed.reshape(seq_count, part_rows, -1)
    mixed_out = lax.all_to_all(summed, "seq", split_axis=0, concat_axis=2, tiled=True)
    return mixed_out.reshape(mixed_out.shape[1], mixed_out.shape[2])


def solution(mesh):
    in_specs = (P("seq", None), P(), P(), P("seq", "tp"), P("seq", "tp"), P("tp", "seq"))
    out_specs = P(("seq", "tp"), None)
    return jax.shard_map(shards, mesh=mesh, in_specs=in_specs, out_specs=out_specs, check_vma=False)
```

time: 410 us -> 259 us (0.63)
  waiting for transfers between devices: 254 us -> 0.01 us
  Pallas kernels: 0 us -> 179 us
  matrix products: 35.5 us -> 0 us
  other arithmetic: 18.6 us -> 2.57 us
  between operations: 13.2 us -> 0.06 us
  local copies, waits for them, and re-layouts: 10.8 us -> 3.3 us
    reduce_scatter x2 -> x0, waiting for transfers between devices: 182 us -> none  [the longest x1 148 us: shards(): lax.psum_scatter(jnp.dot(all_rows, w_both, preferred_element_type=jnp.flo...]
    pallas_call x0 -> x1, Pallas kernels: none -> 179 us  [ffn(): pl.pallas_call(functools.partial(ffn_kernel, seq_n, tp_n), out_shape=jax....]
    all_gather x1 -> x0, waiting for transfers between devices: 71.9 us -> none  [shards(): lax.all_gather(hidden, 'seq', axis=0, tiled=True)]
    dot_general x2 -> x0, matrix products: 35.5 us -> none  [the longest x1 22.3 us: shards(): jnp.dot(all_rows, w_both, preferred_element_type=jnp.float32)]
    all_to_all x1, blocking collectives: 55 us -> 23.4 us  [shards(): lax.all_to_all(normed, 'seq', split_axis=1, concat_axis=0, tiled=True)]
    all_to_all x0 -> x1, blocking collectives: none -> 30 us  [shards(): lax.all_to_all(terms, 'tp', split_axis=0, concat_axis=0, tiled=True)]
    reduce_sum x1, other arithmetic: 8.75 us -> 0.62 us  [shards(): jnp.mean(conv_out * conv_out, axis=-1, keepdims=True) + 1e-05]
    convert_element_type x3 -> x1, other arithmetic: 6.37 us -> 1.35 us  [shards(): extended = lax.dynamic_slice_in_dim(extended, lax.axis_index('tp') * part...]
  transfers between devices with their start and end apart: 4 -> 1, of which waited for: 3 -> 0; matrix products, arithmetic and copies ran while one was open for 1% -> 1% of each run, Pallas kernels for 0% -> 0%
where the time goes in v1:
time: 259 us
  Pallas kernels  179 us (69%)
  blocking collectives  71.1 us (27%)
  local copies, waits for them, and re-layouts  3.3 us (1%)
    pallas_call x1, Pallas kernels, ffn(): pl.pallas_call(functools.partial(ffn_kernel, seq_n, tp_n), out_shape=jax....  179 us
    all_to_all x1, blocking collectives, shards(): lax.all_to_all(terms, 'tp', split_axis=0, concat_axis=0, tiled=True)  30 us
    all_to_all x1, blocking collectives, shards(): lax.all_to_all(normed, 'seq', split_axis=1, concat_axis=0, tiled=True)  23.4 us
    all_to_all x1, blocking collectives, shards(): lax.all_to_all(summed, 'seq', split_axis=0, concat_axis=2, tiled=True)  17.7 us
  transfers between devices with their start and end apart: 1, of which 0 were waited for; matrix products, arithmetic and copies ran while one was open for 1% of the time, Pallas kernels for 0%

profile of v1, /device:TPU:0, one launch (start us, length us, event | category | flops | bytes accessed | tf_op | source)
XLA Modules:
  0.0 258.9 jit_solution(14710042539007248720)
XLA Ops:
  0.0 0.9 slice.28
  0.9 2.4 collective-permute-start
  3.4 1.4 fusion.6
  4.7 0.0 collective-permute-done
  4.7 1.4 fusion.4
  6.1 0.0 copy-start
  6.1 0.6 multiply_reduce_fusion
  6.7 0.1 copy-done
  6.9 0.2 multiply_convert_fusion
  7.1 23.4 %all_to_all.39 = bf16[32,8,1024]{2,0,1:T(8,128)(2,1)} all-to-all(bf16[32,8,1024]{2,0,1:T(8,128)(2,1)S(1)} %bitcast.23), channel_id=1, replica_groups=mesh['seq'=8,'tp'=4] {'seq'}, dimensions={1} | all-to-all | bytes 1048576 | tf_op jit(solution)/shard_map/all_to_all | solution.py:292
  30.4 179.4 %shard_map.64 = bf16[1024,1024]{1,0:T(8,128)(2,1)} custom-call(bf16[256,1024]{1,0:T(8,128)(2,1)} %bitcast.26, bf16[1024,3584]{1,0:T(8,128)(2,1)} %gw_ref.1, bf16[1024,3584]{1,0:T(8,128)(2,1)} %uw_ref.1, bf16[3584,1024]{1,0:T(8,128)(2,1)} %dw_ref.1), custom_call_target="tpu_custom_call" | custom-call | flops 22548578304 | bytes 22020096 | tf_op jit(solution)/shard_map/pallas_call | solution.py:251
  209.9 30.0 %all_to_all.40 = bf16[4,256,1024]{2,1,0:T(8,128)(2,1)S(1)} all-to-all(bf16[4,256,1024]{2,1,0:T(8,128)(2,1)} %bitcast.21), channel_id=1, replica_groups=mesh['seq'=8,'tp'=4] {'tp'}, dimensions={0} | all-to-all | bytes 4194304 | tf_op jit(solution)/shard_map/all_to_all | solution.py:300
  239.9 0.4 reduce_sum.22
  240.3 17.7 %all_to_all.41 = bf16[8,32,1024]{2,1,0:T(8,128)(2,1)S(1)} all-to-all(bf16[8,32,1024]{2,1,0:T(8,128)(2,1)S(1)} %bitcast.25), channel_id=1, replica_groups=mesh['seq'=8,'tp'=4] {'seq'}, dimensions={0} | all-to-all | bytes 1048576 | tf_op jit(solution)/shard_map/all_to_all | solution.py:303
  258.0 0.8 copy.12
  (2 shorter events, 0.0 us)
Async XLA Ops:
  0.9 3.8 %collective-permute-start = (bf16[3,8192]{1,0:T(4,128)(2,1)S(1)}, bf16[3,8192]{1,0:T(4,128)(2,1)S(1)}, u32[]{:S(2)}, u32[]{:S(2)}) collective-permute-start(bf16[3,8192]{1,0:T(4,128)(2,1)S(1)} %slice.28), channel_id=1, source_target_pairs={{0,4},{4,8},{8,12},{12,16},{16,20},{20,24},{24,28},{1,5},{5,9},{9,... | collective-permute-start | bytes 147464 | tf_op jit(solution)/shard_map/ppermute | solution.py:20
  6.1 0.8 copy-start

commit v2 on v1

--- a/solution.py
+++ b/solution.py
@@ -8,10 +8,10 @@
 from jax.sharding import PartitionSpec as P
 
 MESH = pl.DeviceIdType.MESH
-WIDTH = 256
+WIDTH = 128
 BLOCK_TOKENS = 1024
-RS_LAG = 1
-AG_LAG = 1
+RS_LAG = 2
+AG_LAG = 2
 
 
 def from_behind(shard, axis, by):

time: 259 us -> 250 us (0.965)
  Pallas kernels: 179 us -> 170 us
    pallas_call x1, Pallas kernels: 179 us -> 170 us  [ffn(): pl.pallas_call(functools.partial(ffn_kernel, seq_n, tp_n), out_shape=jax....]
where the time goes in v2:
time: 250 us; the launch traced here: 249 us
  Pallas kernels  170 us (68%)
  blocking collectives  71.1 us (28%)
  local copies, waits for them, and re-layouts  3.3 us (1%)
  other arithmetic  2.57 us (1%)
    pallas_call x1, Pallas kernels, ffn(): pl.pallas_call(functools.partial(ffn_kernel, seq_n, tp_n), out_shape=jax....  170 us
    all_to_all x1, blocking collectives, shards(): lax.all_to_all(terms, 'tp', split_axis=0, concat_axis=0, tiled=True)  30 us
    all_to_all x1, blocking collectives, shards(): lax.all_to_all(normed, 'seq', split_axis=1, concat_axis=0, tiled=True)  23.4 us
    all_to_all x1, blocking collectives, shards(): lax.all_to_all(summed, 'seq', split_axis=0, concat_axis=2, tiled=True)  17.7 us
  transfers between devices with their start and end apart: 1, of which 0 were waited for; matrix products, arithmetic and copies ran while one was open for 1% of the time, Pallas kernels for 0%

profile of v2, /device:TPU:0, one launch (start us, length us, event | category | flops | bytes accessed | tf_op | source)
XLA Modules:
  0.0 249.5 jit_solution(12884386518264593264)
XLA Ops:
  0.0 0.9 slice.28
  0.9 2.4 collective-permute-start
  3.4 1.4 fusion.6
  4.7 0.0 collective-permute-done
  4.7 1.4 fusion.4
  6.1 0.0 copy-start
  6.1 0.6 multiply_reduce_fusion
  6.7 0.1 copy-done
  6.9 0.2 multiply_convert_fusion
  7.1 23.4 %all_to_all.39 = bf16[32,8,1024]{2,0,1:T(8,128)(2,1)} all-to-all(bf16[32,8,1024]{2,0,1:T(8,128)(2,1)S(1)} %bitcast.23), channel_id=1, replica_groups=mesh['seq'=8,'tp'=4] {'seq'}, dimensions={1} | all-to-all | bytes 1048576 | tf_op jit(solution)/shard_map/all_to_all | solution.py:292
  30.4 170.0 %shard_map.64 = bf16[1024,1024]{1,0:T(8,128)(2,1)} custom-call(bf16[256,1024]{1,0:T(8,128)(2,1)} %bitcast.26, bf16[1024,3584]{1,0:T(8,128)(2,1)} %gw_ref.1, bf16[1024,3584]{1,0:T(8,128)(2,1)} %uw_ref.1, bf16[3584,1024]{1,0:T(8,128)(2,1)} %dw_ref.1), custom_call_target="tpu_custom_call" | custom-call | flops 22548578304 | bytes 22020096 | tf_op jit(solution)/shard_map/pallas_call | solution.py:251
  200.4 30.0 %all_to_all.40 = bf16[4,256,1024]{2,1,0:T(8,128)(2,1)S(1)} all-to-all(bf16[4,256,1024]{2,1,0:T(8,128)(2,1)} %bitcast.21), channel_id=1, replica_groups=mesh['seq'=8,'tp'=4] {'tp'}, dimensions={0} | all-to-all | bytes 4194304 | tf_op jit(solution)/shard_map/all_to_all | solution.py:300
  230.5 0.4 reduce_sum.22
  230.9 17.7 %all_to_all.41 = bf16[8,32,1024]{2,1,0:T(8,128)(2,1)S(1)} all-to-all(bf16[8,32,1024]{2,1,0:T(8,128)(2,1)S(1)} %bitcast.25), channel_id=1, replica_groups=mesh['seq'=8,'tp'=4] {'seq'}, dimensions={0} | all-to-all | bytes 1048576 | tf_op jit(solution)/shard_map/all_to_all | solution.py:303
  248.6 0.8 copy.12
  (2 shorter events, 0.0 us)
Async XLA Ops:
  0.9 3.8 %collective-permute-start = (bf16[3,8192]{1,0:T(4,128)(2,1)S(1)}, bf16[3,8192]{1,0:T(4,128)(2,1)S(1)}, u32[]{:S(2)}, u32[]{:S(2)}) collective-permute-start(bf16[3,8192]{1,0:T(4,128)(2,1)S(1)} %slice.28), channel_id=1, source_target_pairs={{0,4},{4,8},{8,12},{12,16},{16,20},{20,24},{24,28},{1,5},{5,9},{9,... | collective-permute-start | bytes 147464 | tf_op jit(solution)/shard_map/ppermute | solution.py:20
  6.1 0.8 copy-start
